TPU v7x, 768 devices: a whole 4x8x12 slice. The times are simulated.
768 devices in a mesh: dom: 12 (over z), grp: 64 (over x, y, core).
Axes of the slice: x: 4, y: 8, z: 12, core: 2. Of those that a mesh axis runs over, the one named last changes fastest.
Arguments:
- master_rows: bfloat16 [64, 1536, 512], P('grp', 'dom'), may hold values from -6 to 6
- cotangent: bfloat16 [64, 1536, 512], P('grp', 'dom'), may hold values from -6 to 6
- relation_weight: bfloat16 [4, 512, 512], replicated, may hold values from -0.125 to 0.125
- self_weight: bfloat16 [512, 512], replicated, may hold values from -0.25 to 0.25
- edge_source: int32 [64, 24576], P('grp', 'dom'), may hold values from 0 to 319
- edge_target: int32 [64, 24576], P('grp', 'dom'), may hold values from 0 to 319
- edge_relation: int32 [64, 24576], P('grp', 'dom'), may hold values from 0 to 3
- send_rows: int32 [64, 2304], P('grp', 'dom'), may hold values from 0 to 127
- send_counts: int32 [64, 144], P('grp', 'dom'), may hold values from 4 to 16, as said below
Outputs:
- activation: bfloat16 [64, 1536, 512], P('grp', 'dom')
- input_grad: bfloat16 [64, 1536, 512], P('grp', 'dom')
- weight_grads: float32 [5, 512, 512], P(None, 'grp')
Inputs may be any that keep to these rules, and one draw needn't show every extreme that they name: `send_counts`: on every device the count for some peer is exactly 16.
All inputs are finite; a program needn't handle non-finite values.
Results may differ from a plain program's by a relative error of at most 0.0061.
Values may be sent and summed in bfloat16 or wider, within the bound.
A program may use at most 32 MiB of HBM per device.

v0:
```python
import jax
import jax.numpy as jnp
from jax import lax
from jax.sharding import Mesh
from jax.sharding import PartitionSpec as P

GRP = ("grp_0", "grp_1", "grp_2")


def sum_in_order(parts, axes, sequence):
    lengths = [lax.axis_size(a) for a in axes]
    parts = parts.reshape(*lengths, *parts.shape[1:])
    parts = parts.transpose(*sequence, *range(len(axes), parts.ndim))
    parts = parts.reshape(-1, *parts.shape[len(axes) :])
    for k in sequence:
        parts = lax.psum_scatter(parts, axes[k], scatter_dimension=0, tiled=True)
    return parts[0]


def cut_along(array, dim, devices):
    lengths = array.shape
    parts = array.reshape(*lengths[:dim], devices, lengths[dim] // devices, *lengths[dim + 1 :])
    return jnp.moveaxis(parts, dim, 0)


def summed_rows(array, axes, sequence, dim):
    devices = lax.axis_size(axes)
    return sum_in_order(cut_along(array, dim, devices), axes, sequence)


def from_everyone(array, axis):
    copies = jnp.broadcast_to(array, (lax.axis_size(axis), *array.shape))
    return lax.all_to_all(copies, axis, split_axis=0, concat_axis=0, tiled=True)


def taken_together(array, axis):
    return from_everyone(array, axis).sum(axis=0)


def pull_rows(table, send_rows, valid):
    domains = lax.axis_size("dom")
    width = table.shape[1]
    picked = table[send_rows]
    picked = jnp.where(valid[:, None], picked, jnp.zeros_like(picked))
    moved = lax.all_to_all(
        picked.reshape(domains, -1, width), "dom", split_axis=0, concat_axis=0, tiled=True
    )
    return jnp.concatenate([table, moved.reshape(-1, width)], axis=0)


def push_rows(mirror_part, placement, own):
    domains = lax.axis_size("dom")
    width = own.shape[1]
    moved = lax.all_to_all(
        mirror_part.reshape(domains, -1, width), "dom", split_axis=0, concat_axis=0, tiled=True
    )
    return own + jnp.dot(placement, moved.reshape(-1, width), preferred_element_type=jnp.float32)


def edge_counts(sources, targets, relation, relations, local_rows):
    flat_index = (relation * local_rows + targets) * local_rows + sources
    ones = jnp.ones(sources.shape, jnp.float32)
    counted = jax.ops.segment_sum(
        ones, flat_index, num_segments=relations * local_rows * local_rows
    )
    return counted.reshape(relations, local_rows, local_rows).astype(jnp.bfloat16)


def per_device(
    master_rows,
    cotangent,
    relation_weight,
    self_weight,
    edge_source,
    edge_target,
    edge_relation,
    send_rows,
    send_counts,
):
    masters = master_rows[0]
    cotan = cotangent[0]
    sources = edge_source[0]
    targets = edge_target[0]
    relation = edge_relation[0]
    slots = send_rows[0]
    counts = send_counts[0]
    domains = lax.axis_size("dom")
    relations = relation_weight.shape[0]
    master_count = masters.shape[0]
    capacity = slots.shape[0] // domains
    valid = (jnp.arange(capacity)[None, :] < counts[:, None]).reshape(-1)
    placement = ((slots[None, :] == jnp.arange(master_count)[:, None]) & valid[None, :]).astype(
        jnp.bfloat16
    )
    table = pull_rows(masters, slots, valid)
    local_rows = table.shape[0]
    adjacency = edge_counts(sources, targets, relation, relations, local_rows)
    aggregated = jnp.einsum(
        "rij,jd->rid", adjacency, table, preferred_element_type=jnp.float32
    ).astype(jnp.bfloat16)
    partial_value = jnp.einsum(
        "rnd,rde->ne", aggregated, relation_weight, preferred_element_type=jnp.float32
    )
    own = partial_value[:master_count] + jnp.dot(
        masters, self_weight, preferred_element_type=jnp.float32
    )
    z_value = push_rows(partial_value[master_count:].astype(jnp.bfloat16), placement, own)
    activation = jax.nn.silu(z_value).astype(jnp.bfloat16)
    sigmoid_z = jax.nn.sigmoid(z_value)
    grad_z = (cotan.astype(jnp.float32) * sigmoid_z * (1.0 + z_value * (1.0 - sigmoid_z))).astype(
        jnp.bfloat16
    )
    grad_table = pull_rows(grad_z, slots, valid)
    relation_grad = jnp.einsum(
        "rnd,ne->rde", aggregated, grad_table, preferred_element_type=jnp.float32
    )
    self_grad = jnp.dot(masters.T, grad_z, preferred_element_type=jnp.float32)
    local_grads = jnp.concatenate([relation_grad, self_grad[None]], axis=0)
    group_part = summed_rows(local_grads, GRP, (2, 0, 1), 1)
    weight_grads = taken_together(group_part, "dom")
    back = jnp.einsum(
        "rij,id->rjd", adjacency, grad_table, preferred_element_type=jnp.float32
    ).astype(jnp.bfloat16)
    back_partial = jnp.einsum(
        "rne,rde->nd", back, relation_weight, preferred_element_type=jnp.float32
    )
    back_own = back_partial[:master_count] + jnp.dot(
        grad_z, self_weight.T, preferred_element_type=jnp.float32
    )
    input_grad = push_rows(back_partial[master_count:].astype(jnp.bfloat16), placement, back_own)
    return (activation[None], input_grad.astype(jnp.bfloat16)[None], weight_grads)


def solution(mesh):
    finer = Mesh(
        mesh.devices.reshape(mesh.shape["dom"], 4, 8, 2), ("dom", "grp_0", "grp_1", "grp_2")
    )
    in_specs = (
        P(GRP, "dom", None),
        P(GRP, "dom", None),
        P(),
        P(),
        P(GRP, "dom"),
        P(GRP, "dom"),
        P(GRP, "dom"),
        P(GRP, "dom"),
        P(GRP, "dom"),
    )
    out_specs = (P(GRP, "dom", None), P(GRP, "dom", None), P(None, GRP, None))
    return jax.shard_map(
        per_device, mesh=finer, in_specs=in_specs, out_specs=out_specs, check_vma=False
    )
```

profile of v0, /device:TPU:64, one launch (start us, length us, event | category | flops | bytes accessed | tf_op | source)
XLA Modules:
  0.0 261.0 jit_solution(8887872359778721178)
XLA Ops:
  7.2 0.8 compare_select_fusion
  8.0 0.7 iota_compare_fusion.1
  8.8 2.0 gather_fusion
  10.7 0.8 broadcast_select_fusion.1
  11.5 14.8 %all-to-all-start = ((bf16[12,16,512]{2,1,0:T(8,128)(2,1)}), bf16[12,16,512]{2,1,0:T(8,128)(2,1)S(1)}, u32[]{:S(2)}, u32[]{:S(2)}) async-start(bf16[12,16,512]{2,1,0:T(8,128)(2,1)} %broadcast_select_fusion.1), calls=%async_computation | async-start | bytes 393216 | tf_op jit(solution)/shard_map/all_to_all | solution.py:45
  26.4 12.5 %scatter_custom_fusion = f32[409600]{0:T(1024)} fusion(s32[2048]{0:T(1024)S(1)} %bitcast.75, f32[2048]{0:T(1024)S(1)} %broadcast.65, f32[]{:T(128)} %constant.6.clone.1), kind=kCustom, calls=%fused_computation.16 | custom fusion | flops 2048 | bytes 1638404 | tf_op jit(solution)/shard_map/scatter-add | solution.py:63
  38.9 1.5 convert_element_type.30
  40.4 1.9 convert_element_type.31
  42.3 2.0 convolution_convert_fusion.1
  44.4 0.8 convolution_bitcast_fusion.3
  46.2 9.6 %all-to-all-start.1 = ((bf16[12,16,512]{2,1,0:T(8,128)(2,1)}), bf16[12,16,512]{2,1,0:T(8,128)(2,1)}, u32[]{:S(2)}, u32[]{:S(2)}) async-start(bf16[12,16,512]{2,1,0:T(8,128)(2,1)} %bitcast.10), calls=%async_computation.1 | async-start | bytes 393216 | tf_op jit(solution)/shard_map/all_to_all | solution.py:54
  55.9 0.9 convolution_add_fusion.3
  56.8 12.0 %all-to-all-done.1 = bf16[12,16,512]{2,1,0:T(8,128)(2,1)} async-done(((bf16[12,16,512]{2,1,0:T(8,128)(2,1)}), bf16[12,16,512]{2,1,0:T(8,128)(2,1)}, u32[]{:S(2)}, u32[]{:S(2)}) %all-to-all-start.1) | async-done | bytes 196640 | tf_op jit(solution)/shard_map/all_to_all | solution.py:54
  68.9 2.0 fusion.7
  70.9 1.0 gather_fusion.1
  71.9 0.8 broadcast_select_fusion
  72.7 4.6 %all-to-all-start.2 = ((bf16[12,16,512]{2,1,0:T(8,128)(2,1)}), bf16[12,16,512]{2,1,0:T(8,128)(2,1)}, u32[]{:S(2)}, u32[]{:S(2)}) async-start(bf16[12,16,512]{2,1,0:T(8,128)(2,1)} %broadcast_select_fusion), calls=%async_computation.2 | async-start | bytes 393216 | tf_op jit(solution)/shard_map/all_to_all | solution.py:45
  77.6 11.6 %all-to-all-done.2 = bf16[12,16,512]{2,1,0:T(8,128)(2,1)} async-done(((bf16[12,16,512]{2,1,0:T(8,128)(2,1)}), bf16[12,16,512]{2,1,0:T(8,128)(2,1)}, u32[]{:S(2)}, u32[]{:S(2)}) %all-to-all-start.2) | async-done | bytes 196640 | tf_op jit(solution)/shard_map/all_to_all | solution.py:45
  89.2 2.6 convolution_bitcast_fusion
  92.4 2.9 %copy.23 = f32[2,4,8,5,8,512]{5,4,3,2,1,0:T(8,128)} copy(f32[2,4,8,5,8,512]{5,4,3,0,2,1:T(8,128)S(1)} %bitcast.68) | data formatting | bytes 10485760 | tf_op jit(solution)/shard_map/transpose | solution.py:13
  95.4 19.2 %reduce-scatter.4.cloned.1.call-done = f32[32,5,8,512]{3,2,1,0:T(8,128)} async-done(((f32[64,5,8,512]{3,2,1,0:T(8,128)}), f32[32,5,8,512]{3,2,1,0:T(8,128)}) %reduce-scatter.4.cloned.1.call-update) | async-done | bytes 2621456 | tf_op jit(solution)/shard_map/reduce_scatter | solution.py:16
  114.7 46.5 %reduce-scatter.6.cloned.1.call-done = f32[8,5,8,512]{3,2,1,0:T(8,128)} async-done(((f32[32,5,8,512]{3,2,1,0:T(8,128)}), f32[8,5,8,512]{3,2,1,0:T(8,128)}) %reduce-scatter.6.cloned.1.call-update) | async-done | bytes 655376 | tf_op jit(solution)/shard_map/reduce_scatter | solution.py:16
  161.2 3.4 %convolution_bitcast_fusion.2 = f32[320,512]{1,0:T(8,128)} fusion(bf16[4,512,512]{2,1,0:T(8,128)(2,1)S(1)} %copy-done, bf16[4,320,320]{2,1,0:T(8,128)(2,1)S(1)} %copy-done.4, bf16[192,512]{1,0:T(8,128)(2,1)} %bitcast.15, bf16[128,512]{1,0:T(8,128)(2,1)S(1)} %get-tuple-element.3), kind=kOutput, calls=%fused_computation.8 | convolution fusion | flops 1091829760 | bytes 3899392 | tf_op jit(solution)/shard_map/rne,rde->nd/dot_general | solution.py:124
  164.6 1.0 slice.30
  165.6 23.8 %all_to_all.25 = bf16[12,16,512]{2,1,0:T(8,128)(2,1)S(1)} all-to-all(bf16[12,16,512]{2,1,0:T(8,128)(2,1)S(1)} %bitcast.71), channel_id=1, replica_groups=mesh['dom'=12,'grp_0'=4,'grp_1'=8,'grp_2'=2] {'dom'}, dimensions={0} | all-to-all | bytes 393216 | tf_op jit(solution)/shard_map/all_to_all | solution.py:54
  189.4 17.9 %reduce-scatter.8.cloned.1.call-done = f32[1,5,8,512]{3,2,1,0:T(8,128)} async-done(((f32[8,5,8,512]{3,2,1,0:T(8,128)}), f32[1,5,8,512]{3,2,1,0:T(8,128)}) %reduce-scatter.8.cloned.1.call-update) | async-done | bytes 81936 | tf_op jit(solution)/shard_map/reduce_scatter | solution.py:16
  207.3 2.0 broadcast_in_dim.37
  209.2 10.5 %all-to-all-start.4 = ((f32[12,5,8,512]{3,2,1,0:T(8,128)}), f32[12,5,8,512]{3,2,1,0:T(8,128)S(1)}, u32[]{:S(2)}, u32[]{:S(2)}) async-start(f32[12,5,8,512]{3,2,1,0:T(8,128)} %broadcast_in_dim.37), calls=%async_computation.7 | async-start | bytes 1966080 | tf_op jit(solution)/shard_map/all_to_all | solution.py:33
  219.8 1.4 convolution_add_fusion.1
  221.2 0.8 fusion.1
  222.0 31.7 %all-to-all-done.4 = f32[12,5,8,512]{3,2,1,0:T(8,128)S(1)} async-done(((f32[12,5,8,512]{3,2,1,0:T(8,128)}), f32[12,5,8,512]{3,2,1,0:T(8,128)S(1)}, u32[]{:S(2)}, u32[]{:S(2)}) %all-to-all-start.4) | async-done | bytes 983072 | tf_op jit(solution)/shard_map/all_to_all | solution.py:33
  253.8 0.7 reduce_sum.9
  (32 shorter events, 2.1 us)
Async XLA Ops:
  7.2 37.2 %copy-start = (bf16[4,512,512]{2,1,0:T(8,128)(2,1)S(1)}, bf16[4,512,512]{2,1,0:T(8,128)(2,1)}, u32[]{:S(2)}) copy-start(bf16[4,512,512]{2,1,0:T(8,128)(2,1)} %param.11) | copy-start | bytes 6291460
  7.2 19.1 %copy-start.7 = (s32[1,2048]{1,0:T(1,128)S(1)}, s32[1,2048]{1,0:T(1,128)}, u32[]{:S(2)}) copy-start(s32[1,2048]{1,0:T(1,128)} %param.15) | copy-start | bytes 24580
  7.2 19.1 %copy-start.6 = (s32[1,2048]{1,0:T(1,128)S(1)}, s32[1,2048]{1,0:T(1,128)}, u32[]{:S(2)}) copy-start(s32[1,2048]{1,0:T(1,128)} %param.14) | copy-start | bytes 24580
  7.2 19.1 %copy-start.5 = (s32[1,2048]{1,0:T(1,128)S(1)}, s32[1,2048]{1,0:T(1,128)}, u32[]{:S(2)}) copy-start(s32[1,2048]{1,0:T(1,128)} %param.13) | copy-start | bytes 24580
  11.5 30.8 %all-to-all-start = ((bf16[12,16,512]{2,1,0:T(8,128)(2,1)}), bf16[12,16,512]{2,1,0:T(8,128)(2,1)S(1)}, u32[]{:S(2)}, u32[]{:S(2)}) async-start(bf16[12,16,512]{2,1,0:T(8,128)(2,1)} %broadcast_select_fusion.1), calls=%async_computation | async-start | bytes 393216 | tf_op jit(solution)/shard_map/all_to_all | solution.py:45
  38.9 3.5 %copy-start.1 = (bf16[1,128,512]{2,1,0:T(8,128)(2,1)S(1)}, bf16[1,128,512]{2,1,0:T(8,128)(2,1)}, u32[]{:S(2)}) copy-start(bf16[1,128,512]{2,1,0:T(8,128)(2,1)} %param.9) | copy-start | bytes 393220
  44.4 1.1 copy-start.3
  44.4 11.5 %copy-start.2 = (bf16[512,512]{1,0:T(8,128)(2,1)S(1)}, bf16[512,512]{1,0:T(8,128)(2,1)}, u32[]{:S(2)}) copy-start(bf16[512,512]{1,0:T(8,128)(2,1)} %param.12) | copy-start | bytes 1572868
  44.4 24.4 %copy-start.8 = (s32[1,192]{1,0:T(1,128)S(1)}, s32[1,192]{1,0:T(1,128)}, u32[]{:S(2)}) copy-start(s32[1,192]{1,0:T(1,128)} %param.16) | copy-start | bytes 2308
  46.2 22.7 %all-to-all-start.1 = ((bf16[12,16,512]{2,1,0:T(8,128)(2,1)}), bf16[12,16,512]{2,1,0:T(8,128)(2,1)}, u32[]{:S(2)}, u32[]{:S(2)}) async-start(bf16[12,16,512]{2,1,0:T(8,128)(2,1)} %bitcast.10), calls=%async_computation.1 | async-start | bytes 393216 | tf_op jit(solution)/shard_map/all_to_all | solution.py:54
  72.7 16.5 %all-to-all-start.2 = ((bf16[12,16,512]{2,1,0:T(8,128)(2,1)}), bf16[12,16,512]{2,1,0:T(8,128)(2,1)}, u32[]{:S(2)}, u32[]{:S(2)}) async-start(bf16[12,16,512]{2,1,0:T(8,128)(2,1)} %broadcast_select_fusion), calls=%async_computation.2 | async-start | bytes 393216 | tf_op jit(solution)/shard_map/all_to_all | solution.py:45
  77.3 37.4 %reduce-scatter.4.cloned.1.call-start = ((), (), s32[]{:S(2)}) async-start(), calls=%async_computation.8 | async-start | bytes 7864320 | tf_op jit(solution)/shard_map/reduce_scatter | solution.py:16
  95.3 65.9 %copy-start.4 = (bf16[4,320,320]{2,1,0:T(8,128)(2,1)S(1)}, bf16[4,320,320]{2,1,0:T(8,128)(2,1)}, u32[]{:S(2)}) copy-start(bf16[4,320,320]{2,1,0:T(8,128)(2,1)} %convert_element_type.31) | copy-start | bytes 2457604
  95.3 65.9 %reduce-scatter.6.cloned.1.call-start = ((), (), s32[]{:S(2)}) async-start(), calls=%async_computation.9 | async-start | bytes 3276800 | tf_op jit(solution)/shard_map/reduce_scatter | solution.py:16
  114.6 92.6 %reduce-scatter.8.cloned.1.call-start = ((), (), s32[]{:S(2)}) async-start(), calls=%async_computation.10 | async-start | bytes 737280 | tf_op jit(solution)/shard_map/reduce_scatter | solution.py:16
  209.2 44.5 %all-to-all-start.4 = ((f32[12,5,8,512]{3,2,1,0:T(8,128)}), f32[12,5,8,512]{3,2,1,0:T(8,128)S(1)}, u32[]{:S(2)}, u32[]{:S(2)}) async-start(f32[12,5,8,512]{3,2,1,0:T(8,128)} %broadcast_in_dim.37), calls=%async_computation.7 | async-start | bytes 1966080 | tf_op jit(solution)/shard_map/all_to_all | solution.py:33
Sparse Core Ops, SparseCore 0:
  95.4 19.1 reduce-scatter.3
  117.8 43.3 reduce-scatter.5
  164.3 42.9 reduce-scatter.7
where the time goes:
time: 262 us; the launch traced here: 261 us
  waiting for transfers between devices  139 us (53%)
  starting transfers between devices  39.6 us (15%)
  blocking collectives  23.8 us (9%)
  other arithmetic  18.5 us (7%)
  matrix products  14.4 us (5%)
  between operations  13.9 us (5%)
  local copies, waits for them, and re-layouts  11.8 us (5%)
    reduce_scatter x3, waiting for transfers between devices, sum_in_order(): parts = lax.psum_scatter(parts, axes[k], scatter_dimension=0, tiled=True)  83.6 us
    all_to_all x1, waiting for transfers between devices, from_everyone(): return lax.all_to_all(copies, axis, split_axis=0, concat_axis=0, tiled=True)  31.7 us
    all_to_all x1, blocking collectives, push_rows(): lax.all_to_all(mirror_part.reshape(domains, -1, width), 'dom', split_axis...  23.8 us
    all_to_all x2, starting transfers between devices, pull_rows(): lax.all_to_all(picked.reshape(domains, -1, width), 'dom', split_axis=0, c...  19.4 us
    scatter-add x1, other arithmetic, edge_counts(): jax.ops.segment_sum(ones, flat_index, num_segments=relations * local_rows...  12.5 us
    all_to_all x1, waiting for transfers between devices, push_rows(): lax.all_to_all(mirror_part.reshape(domains, -1, width), 'dom', split_axis...  12 us
    all_to_all x2, waiting for transfers between devices, pull_rows(): lax.all_to_all(picked.reshape(domains, -1, width), 'dom', split_axis=0, c...  11.6 us
    all_to_all x1, starting transfers between devices, from_everyone(): return lax.all_to_all(copies, axis, split_axis=0, concat_axis=0, tiled=True)  10.5 us
  transfers between devices with their start and end apart: 7, of which 6 were waited for; matrix products, arithmetic and copies ran while one was open for 9% of the time, Pallas kernels for 0%

commit v1 on v0

v1 whole, which is shorter than its diff:
```python
import functools

import jax
import jax.numpy as jnp
from jax import lax
from jax.experimental import pallas as pl
from jax.experimental.pallas import tpu as pltpu
from jax.sharding import Mesh
from jax.sharding import PartitionSpec as P

GRP = ("grp_0", "grp_1", "grp_2")
MESH = pl.DeviceIdType.MESH
F32 = jnp.float32
BF16 = jnp.bfloat16


def dot(a, b):
    return jnp.dot(a, b, preferred_element_type=F32)


def dot_nt(a, b):
    return lax.dot_general(a, b, (((1,), (1,)), ((), ())), preferred_element_type=F32)


def nearest_last(n):
    return sorted(range(1, n), key=lambda k: (-min(k, n - k), k))


def kernel(
    nz, ny, cap,
    counts_hbm, masters_hbm, cotan_hbm, source_hbm, target_hbm, relation_hbm, slots_hbm, relw_hbm, selfw_hbm,
    act_ref, ingrad_ref, wgrad_ref,
    counts, cotan, source, target, relation, slots, relw, selfw, one_hot, adj, adj_t, place, pick, table, agg, agg_t,
    psend, qsend, qrecv, own, gsend, gtab, back, bown, bsend, brecv, csend, crecv, lg, xs, xr, xt, ysend, ymine, yr,
    zsend, zrecv, zown, wrecv,
    in_sem, s_pull, r_pull, s_push, r_push, s_gpull, r_gpull, s_back, r_back, s_core, r_core, s_x, r_x, s_y, r_y,
    s_z, r_z, s_w, r_w,
):
    z = lax.axis_index("dom")
    x = lax.axis_index("grp_0")
    y = lax.axis_index("grp_1")
    c = lax.axis_index("grp_2")
    nx = 4
    rel = relw.shape[0]
    width = relw.shape[1]
    half = width // 2
    mast = cotan.shape[0]
    rows = table.shape[0]
    mirrors = rows - mast
    piece = width // (nx * ny * 2)
    ring = nearest_last(nz)
    yring = nearest_last(ny)
    sent = []

    def zp(k):
        return lax.rem(z + k, nz)

    def send(copy):
        copy.start()
        sent.append(copy)

    def remote(src, dst, send_sem, recv_sem, **device):
        return pltpu.make_async_remote_copy(
            src_ref=src, dst_ref=dst, send_sem=send_sem, recv_sem=recv_sem, device_id=device, device_id_type=MESH
        )

    barrier = pltpu.get_barrier_semaphore()
    met = [{"dom": zp(k)} for k in ring] + [{"grp_1": lax.rem(y + k, ny)} for k in yring]
    met += [{"grp_0": lax.rem(x + k, nx)} for k in (1, 3)] + [{"grp_2": 1 - c}]
    for device in met:
        pl.semaphore_signal(barrier, inc=1, device_id=device, device_id_type=MESH)

    brought = (
        (counts_hbm, counts), (slots_hbm, slots), (masters_hbm.at[0], table.at[:mast]), (target_hbm, target),
        (source_hbm, source), (relation_hbm, relation), (relw_hbm, relw), (selfw_hbm, selfw),
        (cotan_hbm.at[0], cotan),
    )
    inputs = [pltpu.make_async_copy(a, b, in_sem.at[i]) for i, (a, b) in enumerate(brought)]
    for copy in inputs:
        copy.start()
    for copy in inputs[:2]:
        copy.wait()

    lane = lax.broadcasted_iota(jnp.int32, (1, mirrors), 1)
    limit = jnp.zeros((1, mirrors), jnp.int32)
    for p in range(nz):
        limit = jnp.where((lane >= p * cap) & (lane < (p + 1) * cap), counts[0, p] + p * cap, limit)
    named = jnp.where(lane < limit, slots[...], -1)
    row = lax.broadcasted_iota(jnp.int32, (mast, mirrors), 0)
    placement = jnp.where(row == named, 1.0, 0.0)
    place[...] = placement.astype(BF16)
    pick[...] = placement.T.astype(BF16)

    inputs[2].wait()
    psend[...] = dot(pick[...], table[:mast, :]).astype(BF16).reshape(nz, cap, width)

    def mirror_rows():
        return pl.ds(pl.multiple_of(mast + z * cap, cap), cap)

    def pull(k):
        return remote(psend.at[zp(k)], table.at[mirror_rows(), :], s_pull.at[k], r_pull.at[k], dom=zp(k))

    pl.semaphore_wait(barrier, len(met))
    for k in ring:
        send(pull(k))
    table[mirror_rows(), :] = psend[z]

    for copy in inputs[3:6]:
        copy.wait()
    row = lax.broadcasted_iota(jnp.int32, (rows, source.shape[1]), 0)

    def counted(dst, first, second):
        one_hot[...] = jnp.where(row == second, 1.0, 0.0).astype(BF16)

        @pl.loop(0, rel)
        def _(r):
            mine = jnp.where(relation[...] == r, first, -1)
            hot = jnp.where(row == mine, 1.0, 0.0).astype(BF16)
            dst[pl.ds(pl.multiple_of(r * rows, rows), rows), :] = dot_nt(hot, one_hot[...]).astype(BF16)

    counted(adj, target[...], source[...])
    for copy in inputs[6:]:
        copy.wait()

    for k in ring:
        pull(k).wait_recv()
    agg[...] = dot(adj[...], table[...]).astype(BF16)

    def push(h, k):
        return remote(qsend.at[h, zp(k)], qrecv.at[h, z], s_push.at[h, k], r_push.at[h, k], dom=zp(k))

    for h in (0, 1):
        cols = slice(h * half, (h + 1) * half)
        part = dot(agg[mast:rows, :], relw[0, :, cols])
        for r in range(1, rel):
            part += dot(agg[r * rows + mast : (r + 1) * rows, :], relw[r, :, cols])
        qsend[h] = part.astype(BF16).reshape(nz, cap, half)
        qrecv[h, z] = qsend[h, z]
        for k in ring:
            send(push(h, k))

    for h in (0, 1):
        cols = slice(h * half, (h + 1) * half)
        part = dot(table[:mast, :], selfw[:, cols])
        for r in range(rel):
            part += dot(agg[r * rows : r * rows + mast, :], relw[r, :, cols])
        own[h] = part

    def transposed(values):
        turned = values.astype(F32).T.reshape(nx * ny, 2, piece, values.shape[0])
        return [turned[:, core].reshape(half, values.shape[0]).astype(BF16) for core in (0, 1)]

    for r in range(rel):
        for core, values in enumerate(transposed(agg[r * rows : (r + 1) * rows, :])):
            agg_t[r, core] = values
    for core, values in enumerate(transposed(table[:mast, :])):
        agg_t[rel, core, :, :mast] = values

    counted(adj_t, source[...], target[...])

    def gpull(h, k):
        return remote(gsend.at[h, zp(k)], gtab.at[h, mirror_rows(), :], s_gpull.at[h, k], r_gpull.at[h, k], dom=zp(k))

    for h in (0, 1):
        for k in ring:
            push(h, k).wait_recv()
        cols = slice(h * half, (h + 1) * half)
        value = own[h] + dot(place[...], qrecv[h].reshape(mirrors, half))
        gate = 1.0 / (1.0 + jnp.exp(-value))
        grad = cotan[:, cols].astype(F32) * gate * (1.0 + value * (1.0 - gate))
        gtab[h, :mast, :] = grad.astype(BF16)
        gsend[h] = dot(pick[...], gtab[h, :mast, :]).astype(BF16).reshape(nz, cap, half)
        for k in ring:
            send(gpull(h, k))
        gtab[h, mirror_rows(), :] = gsend[h, z]
        act_ref[0, :, cols] = (value * gate).astype(BF16)

    def to_core(h, r):
        return remote(csend.at[h, r], crecv.at[h, r], s_core.at[h, r], r_core.at[h, r], grp_2=1 - c)

    def local(h, r):
        seen = mast if r == rel else rows
        csend[h, r] = dot(agg_t[r, 1 - c, :, :seen], gtab[h, :seen, :]).astype(BF16)
        send(to_core(h, r))
        lg[h, r] = dot(agg_t[r, c, :, :seen], gtab[h, :seen, :])

    mrow = half // nx
    quarter = mrow // 2

    def block(owner, part):
        return pl.ds(pl.multiple_of(lax.rem(owner, nx) * mrow + part * quarter, quarter), quarter)

    def along_x(h, r, m):
        to, src = (
            (1, xs.at[h, r, block(x + 1, 1), :]),
            (1, xs.at[h, r, block(x + 2, 0), :]),
            (3, xs.at[h, r, block(x + 3, 0), :]),
            (3, xs.at[h, r, block(x + 2, 1), :]),
            (1, xt.at[h, r, 0]),
            (3, xt.at[h, r, 1]),
        )[m]
        return remote(src, xr.at[h, r, m], s_x.at[h, r, m], r_x.at[h, r, m], grp_0=lax.rem(x + to, nx))

    def first_x(h, r):
        to_core(h, r).wait_recv()
        lg[h, r] = lg[h, r] + crecv[h, r].astype(F32)
        xs[h, r] = lg[h, r].astype(BF16)
        for m in (1, 3, 0, 2):
            send(along_x(h, r, m))

    def second_x(h, r):
        along_x(h, r, 1).wait_recv()
        xt[h, r, 0] = (lg[h, r, block(x + 1, 0), :] + xr[h, r, 1].astype(F32)).astype(BF16)
        send(along_x(h, r, 4))
        along_x(h, r, 3).wait_recv()
        xt[h, r, 1] = (lg[h, r, block(x + 3, 1), :] + xr[h, r, 3].astype(F32)).astype(BF16)
        send(along_x(h, r, 5))

    def along_y(h, r, k):
        to = lax.rem(y + k, ny)
        return remote(ysend.at[h, r, to], yr.at[h, r, k], s_y.at[h, r, k], r_y.at[h, r, k], grp_1=to)

    def over_y(h, r):
        for m in (2, 4, 0, 5):
            along_x(h, r, m).wait_recv()
        ymine[h, r, :quarter, :] = lg[h, r, block(x, 0), :] + xr[h, r, 2].astype(F32) + xr[h, r, 4].astype(F32)
        ymine[h, r, quarter:, :] = lg[h, r, block(x, 1), :] + xr[h, r, 0].astype(F32) + xr[h, r, 5].astype(F32)
        ysend[h, r] = ymine[h, r].reshape(ny, piece, half).astype(BF16)
        for k in yring:
            send(along_y(h, r, k))

    parts = 2 * (rel + 1)
    held = -(-parts // nz)

    def along_z(q):
        k = lax.rem(q - z + 2 * nz, nz)
        return remote(zsend.at[q], zrecv.at[q // nz, k], s_z.at[q], r_z.at[q // nz, k], dom=q % nz)

    def over_z(h, r):
        q = 2 * r + h
        total = ymine[h, r, pl.ds(pl.multiple_of(y * piece, piece), piece), :]
        for k in yring:
            along_y(h, r, k).wait_recv()
            total += yr[h, r, k].astype(F32)
        zsend[q] = total

        @pl.when(z != q % nz)
        def _():
            along_z(q).start()

    def units(h):
        return [(h, r) for r in range(rel)]

    first = [(0, rel), (1, rel)]
    for u in first:
        local(*u)
    for u in first:
        first_x(*u)

    for k in ring:
        gpull(0, k).wait_recv()
    for u in units(0):
        local(*u)
    for u in units(0):
        first_x(*u)
    for u in first:
        second_x(*u)

    for k in ring:
        gpull(1, k).wait_recv()
    for u in units(1):
        local(*u)
    for u in units(1):
        first_x(*u)
    for u in first:
        over_y(*u)
    for u in units(0):
        second_x(*u)

    for h in (0, 1):
        back[:, h * half : (h + 1) * half] = dot(adj_t[...], gtab[h]).astype(BF16)
    part = dot_nt(back[mast:rows, :], relw[0])
    for r in range(1, rel):
        part += dot_nt(back[r * rows + mast : (r + 1) * rows, :], relw[r])
    bsend[...] = part.astype(BF16).reshape(nz, cap, width)
    brecv[z] = bsend[z]

    def bpush(k):
        return remote(bsend.at[zp(k)], brecv.at[z], s_back.at[k], r_back.at[k], dom=zp(k))

    for k in ring:
        send(bpush(k))

    for u in units(0):
        over_y(*u)
    for u in units(1):
        second_x(*u)
    for u in first:
        over_z(*u)

    part = dot_nt(gtab[0, :mast, :], selfw[:, :half]) + dot_nt(gtab[1, :mast, :], selfw[:, half:])
    for r in range(rel):
        part += dot_nt(back[r * rows : r * rows + mast, :], relw[r])
    bown[...] = part

    for u in units(1):
        over_y(*u)
    for u in units(0):
        over_z(*u)

    for k in ring:
        bpush(k).wait_recv()
    ingrad_ref[0] = (bown[...] + dot(place[...], brecv[...].reshape(mirrors, width))).astype(BF16)

    for u in units(1):
        over_z(*u)

    def shared(i, k):
        q = z + i * nz
        return remote(zown.at[i], wrecv.at[q], s_w.at[i, k], r_w.at[q], dom=zp(k))

    for i in range(held):
        q = z + i * nz

        @pl.when(q < parts)
        def _():
            total = zsend[q]
            for k in range(1, nz):
                remote(zsend.at[0], zrecv.at[i, k], s_z.at[0], r_z.at[i, k], dom=zp(1)).wait_recv()
                total += zrecv[i, k]
            zown[i] = total
            for k in ring:
                shared(i, k).start()
            wrecv[q] = total

    for q in range(parts):
        @pl.when(z != q % nz)
        def _():
            remote(zown.at[0], wrecv.at[q], s_w.at[0, 0], r_w.at[q], dom=zp(1)).wait_recv()

        h = q % 2
        wgrad_ref[q // 2, :, h * half : (h + 1) * half] = wrecv[q]

    for copy in sent:
        copy.wait_send()
    for q in range(parts):
        @pl.when(z != q % nz)
        def _():
            along_z(q).wait_send()
    for i in range(held):
        @pl.when(z + i * nz < parts)
        def _():
            for k in ring:
                shared(i, k).wait_send()


def handed_on(*refs):
    half = len(refs) // 2
    for a, b in zip(refs[:half], refs[half:]):
        b[...] = a[...]


def per_device(
    master_rows, cotangent, relation_weight, self_weight, edge_source, edge_target, edge_relation, send_rows,
    send_counts,
):
    nz = lax.axis_size("dom")
    ny = lax.axis_size("grp_1")
    rel, width = relation_weight.shape[:2]
    mast = master_rows.shape[1]
    mirrors = send_rows.shape[1]
    cap = mirrors // nz
    rows = mast + mirrors
    edges = edge_source.shape[1]
    half = width // 2
    mrow = half // 4
    piece = width // (4 * ny * 2)
    parts = 2 * (rel + 1)
    held = -(-parts // nz)
    vmem = pl.BlockSpec(memory_space=pltpu.VMEM)
    hbm = pl.BlockSpec(memory_space=pl.ANY)
    dma = pltpu.SemaphoreType.DMA
    scratch = [
        pltpu.SMEM((1, nz), jnp.int32),
        pltpu.VMEM((mast, width), BF16),
        pltpu.VMEM((1, edges), jnp.int32),
        pltpu.VMEM((1, edges), jnp.int32),
        pltpu.VMEM((1, edges), jnp.int32),
        pltpu.VMEM((1, mirrors), jnp.int32),
        pltpu.VMEM((rel, width, width), BF16),
        pltpu.VMEM((width, width), BF16),
        pltpu.VMEM((rows, edges), BF16),
        pltpu.VMEM((rel * rows, rows), BF16),
        pltpu.VMEM((rel * rows, rows), BF16),
        pltpu.VMEM((mast, mirrors), BF16),
        pltpu.VMEM((mirrors, mast), BF16),
        pltpu.VMEM((rows, width), BF16),
        pltpu.VMEM((rel * rows, width), BF16),
        pltpu.VMEM((rel + 1, 2, half, rows), BF16),
        pltpu.VMEM((nz, cap, width), BF16),
        pltpu.VMEM((2, nz, cap, half), BF16),
        pltpu.VMEM((2, nz, cap, half), BF16),
        pltpu.VMEM((2, mast, half), F32),
        pltpu.VMEM((2, nz, cap, half), BF16),
        pltpu.VMEM((2, rows, half), BF16),
        pltpu.VMEM((rel * rows, width), BF16),
        pltpu.VMEM((mast, width), F32),
        pltpu.VMEM((nz, cap, width), BF16),
        pltpu.VMEM((nz, cap, width), BF16),
        pltpu.VMEM((2, rel + 1, half, half), BF16),
        pltpu.VMEM((2, rel + 1, half, half), BF16),
        pltpu.VMEM((2, rel + 1, half, half), F32),
        pltpu.VMEM((2, rel + 1, half, half), BF16),
        pltpu.VMEM((2, rel + 1, 6, mrow // 2, half), BF16),
        pltpu.VMEM((2, rel + 1, 2, mrow // 2, half), BF16),
        pltpu.VMEM((2, rel + 1, ny, piece, half), BF16),
        pltpu.VMEM((2, rel + 1, mrow, half), F32),
        pltpu.VMEM((2, rel + 1, ny, piece, half), BF16),
        pltpu.VMEM((parts, piece, half), F32),
        pltpu.VMEM((held, nz, piece, half), F32),
        pltpu.VMEM((held, piece, half), F32),
        pltpu.VMEM((parts, piece, half), F32),
        dma((9,)),
        dma((nz,)), dma((nz,)),
        dma((2, nz)), dma((2, nz)),
        dma((2, nz)), dma((2, nz)),
        dma((nz,)), dma((nz,)),
        dma((2, rel + 1)), dma((2, rel + 1)),
        dma((2, rel + 1, 6)), dma((2, rel + 1, 6)),
        dma((2, rel + 1, ny)), dma((2, rel + 1, ny)),
        dma((parts,)), dma((held, nz)),
        dma((held, nz)), dma((parts,)),
    ]
    out_shape = (
        jax.ShapeDtypeStruct((1, mast, width), BF16),
        jax.ShapeDtypeStruct((1, mast, width), BF16),
        jax.ShapeDtypeStruct((rel + 1, piece, width), F32),
    )
    results = pl.pallas_call(
        functools.partial(kernel, nz, ny, cap),
        out_shape=tuple(pltpu.VMEM(o.shape, o.dtype) for o in out_shape),
        in_specs=[hbm] * 9,
        out_specs=(vmem, vmem, vmem),
        scratch_shapes=scratch,
        compiler_params=pltpu.CompilerParams(
            collective_id=0, has_side_effects=True, vmem_limit_bytes=56 * 1024 * 1024
        ),
        name="graph_conv_step",
    )(
        send_counts, master_rows, cotangent, edge_source, edge_target, edge_relation, send_rows, relation_weight,
        self_weight,
    )
    return pl.pallas_call(
        handed_on,
        out_shape=out_shape,
        in_specs=[vmem] * 3,
        out_specs=(vmem, vmem, vmem),
        compiler_params=pltpu.CompilerParams(vmem_limit_bytes=4 * 1024 * 1024),
        name="handed_on",
    )(*results)


def solution(mesh):
    devices = mesh.devices.shape[1]
    finer = Mesh(
        mesh.devices.reshape(mesh.shape["dom"], 4, devices // 8, 2), ("dom", "grp_0", "grp_1", "grp_2")
    )
    in_specs = (
        P(GRP, "dom", None),
        P(GRP, "dom", None),
        P(),
        P(),
        P(GRP, "dom"),
        P(GRP, "dom"),
        P(GRP, "dom"),
        P(GRP, "dom"),
        P(GRP, "dom"),
    )
    out_specs = (P(GRP, "dom", None), P(GRP, "dom", None), P(None, GRP, None))
    return jax.shard_map(per_device, mesh=finer, in_specs=in_specs, out_specs=out_specs, check_vma=False)
```

time: 262 us -> 81.5 us (0.31)
  the two profiles are of different devices: /device:TPU:64 before, /device:TPU:8 now
where the time goes in v1:
time: 81.5 us; the launch traced here: 81.4 us
  Pallas kernels  80.7 us (99%)
    pallas_call x1, Pallas kernels, per_device(): pl.pallas_call(functools.partial(kernel, nz, ny, cap), out_shape=tuple((p...  80 us

profile of v1, /device:TPU:8, one launch (start us, length us, event | category | flops | bytes accessed | tf_op | source)
XLA Modules:
  0.0 81.4 jit_solution(4760073937759290722)
XLA Ops:
  0.6 80.0 %graph_conv_step.1 = (bf16[1,128,512]{2,1,0:T(8,128)(2,1)S(1)}, bf16[1,128,512]{2,1,0:T(8,128)(2,1)S(1)}, f32[5,8,512]{2,1,0:T(8,128)S(1)}) custom-call(s32[1,12]{1,0:T(1,128)} %counts_hbm.1, bf16[1,128,512]{2,1,0:T(8,128)(2,1)} %masters_hbm.1, bf16[1,128,512]{2,1,0:T(8,128)(2,1)} %cotan_hbm.1, s32[1,2048]{1,0:T(1,128)} %source_hbm.1, s32[1,2048]{1,0:T(1,128)} %target_hbm.1, ...), custom_call_target="tpu_custom_call" | custom-call | tf_op jit(solution)/shard_map/graph_conv_step/pallas_call | solution.py:439
  80.6 0.7 handed_on.1

commit v2 on v1

--- a/solution.py
+++ b/solution.py
@@ -10,6 +10,8 @@
 
 GRP = ("grp_0", "grp_1", "grp_2")
 MESH = pl.DeviceIdType.MESH
+NX = 4
+GROUP = 4
 F32 = jnp.float32
 BF16 = jnp.bfloat16
 
@@ -31,8 +33,8 @@
     counts_hbm, masters_hbm, cotan_hbm, source_hbm, target_hbm, relation_hbm, slots_hbm, relw_hbm, selfw_hbm,
     act_ref, ingrad_ref, wgrad_ref,
     counts, cotan, source, target, relation, slots, relw, selfw, one_hot, adj, adj_t, place, pick, table, agg, agg_t,
-    psend, qsend, qrecv, own, gsend, gtab, back, bown, bsend, brecv, csend, crecv, lg, xs, xr, xt, ysend, ymine, yr,
-    zsend, zrecv, zown, wrecv,
+    psend, qsend, qrecv, own, gsend, gtab, back, bown, bsend, brecv, csend, crecv, lg, xs, xr, ysend, ymine, yr,
+    zmine, zsend, zrecv, zown, wrecv,
     in_sem, s_pull, r_pull, s_push, r_push, s_gpull, r_gpull, s_back, r_back, s_core, r_core, s_x, r_x, s_y, r_y,
     s_z, r_z, s_w, r_w,
 ):
@@ -40,10 +42,11 @@
     x = lax.axis_index("grp_0")
     y = lax.axis_index("grp_1")
     c = lax.axis_index("grp_2")
-    nx = 4
+    nx = NX
     rel = relw.shape[0]
     width = relw.shape[1]
     half = width // 2
+    slab = width // 4
     mast = cotan.shape[0]
     rows = table.shape[0]
     mirrors = rows - mast
@@ -66,7 +69,7 @@
 
     barrier = pltpu.get_barrier_semaphore()
     met = [{"dom": zp(k)} for k in ring] + [{"grp_1": lax.rem(y + k, ny)} for k in yring]
-    met += [{"grp_0": lax.rem(x + k, nx)} for k in (1, 3)] + [{"grp_2": 1 - c}]
+    met += [{"grp_0": lax.rem(x + k, nx)} for k in range(1, nx)] + [{"grp_2": 1 - c}]
     for device in met:
         pl.semaphore_signal(barrier, inc=1, device_id=device, device_id_type=MESH)
 
@@ -124,27 +127,35 @@
 
     for k in ring:
         pull(k).wait_recv()
-    agg[...] = dot(adj[...], table[...]).astype(BF16)
-
-    def push(h, k):
-        return remote(qsend.at[h, zp(k)], qrecv.at[h, z], s_push.at[h, k], r_push.at[h, k], dom=zp(k))
+    for r in range(rel):
+        some = slice(r * rows + mast, (r + 1) * rows)
+        agg[some, :] = dot(adj[some, :], table[...]).astype(BF16)
+
+    def push(b, k):
+        return remote(qsend.at[b, zp(k)], qrecv.at[b, z], s_push.at[b, k], r_push.at[b, k], dom=zp(k))
 
     for h in (0, 1):
         cols = slice(h * half, (h + 1) * half)
         part = dot(agg[mast:rows, :], relw[0, :, cols])
         for r in range(1, rel):
             part += dot(agg[r * rows + mast : (r + 1) * rows, :], relw[r, :, cols])
-        qsend[h] = part.astype(BF16).reshape(nz, cap, half)
-        qrecv[h, z] = qsend[h, z]
-        for k in ring:
-            send(push(h, k))
+        for b in (2 * h, 2 * h + 1):
+            qsend[b] = part[:, (b % 2) * slab : (b % 2 + 1) * slab].astype(BF16).reshape(nz, cap, slab)
+            qrecv[b, z] = qsend[b, z]
+            for k in ring:
+                send(push(b, k))
+
+    for r in range(rel):
+        some = slice(r * rows, r * rows + mast)
+        agg[some, :] = dot(adj[some, :], table[...]).astype(BF16)
 
     for h in (0, 1):
         cols = slice(h * half, (h + 1) * half)
         part = dot(table[:mast, :], selfw[:, cols])
         for r in range(rel):
             part += dot(agg[r * rows : r * rows + mast, :], relw[r, :, cols])
-        own[h] = part
+        own[2 * h] = part[:, :slab]
+        own[2 * h + 1] = part[:, slab:]
 
     def transposed(values):
         turned = values.astype(F32).T.reshape(nx * ny, 2, piece, values.shape[0])
@@ -158,21 +169,23 @@
 
     counted(adj_t, source[...], target[...])
 
-    def gpull(h, k):
-        return remote(gsend.at[h, zp(k)], gtab.at[h, mirror_rows(), :], s_gpull.at[h, k], r_gpull.at[h, k], dom=zp(k))
-
-    for h in (0, 1):
+    def gpull(b, k):
+        at = gtab.at[b // 2, mirror_rows(), pl.ds((b % 2) * slab, slab)]
+        return remote(gsend.at[b, zp(k)], at, s_gpull.at[b, k], r_gpull.at[b, k], dom=zp(k))
+
+    for b in range(4):
         for k in ring:
-            push(h, k).wait_recv()
-        cols = slice(h * half, (h + 1) * half)
-        value = own[h] + dot(place[...], qrecv[h].reshape(mirrors, half))
+            push(b, k).wait_recv()
+        cols = slice(b * slab, (b + 1) * slab)
+        part_cols = slice((b % 2) * slab, (b % 2 + 1) * slab)
+        value = own[b] + dot(place[...], qrecv[b].reshape(mirrors, slab))
         gate = 1.0 / (1.0 + jnp.exp(-value))
-        grad = cotan[:, cols].astype(F32) * gate * (1.0 + value * (1.0 - gate))
-        gtab[h, :mast, :] = grad.astype(BF16)
-        gsend[h] = dot(pick[...], gtab[h, :mast, :]).astype(BF16).reshape(nz, cap, half)
+        grad = (cotan[:, cols].astype(F32) * gate * (1.0 + value * (1.0 - gate))).astype(BF16)
+        gsend[b] = dot(pick[...], grad).astype(BF16).reshape(nz, cap, slab)
         for k in ring:
-            send(gpull(h, k))
-        gtab[h, mirror_rows(), :] = gsend[h, z]
+            send(gpull(b, k))
+        gtab[b // 2, :mast, part_cols] = grad
+        gtab[b // 2, mirror_rows(), part_cols] = gsend[b, z]
         act_ref[0, :, cols] = (value * gate).astype(BF16)
 
     def to_core(h, r):
@@ -185,68 +198,80 @@
         lg[h, r] = dot(agg_t[r, c, :, :seen], gtab[h, :seen, :])
 
     mrow = half // nx
-    quarter = mrow // 2
-
-    def block(owner, part):
-        return pl.ds(pl.multiple_of(lax.rem(owner, nx) * mrow + part * quarter, quarter), quarter)
-
-    def along_x(h, r, m):
-        to, src = (
-            (1, xs.at[h, r, block(x + 1, 1), :]),
-            (1, xs.at[h, r, block(x + 2, 0), :]),
-            (3, xs.at[h, r, block(x + 3, 0), :]),
-            (3, xs.at[h, r, block(x + 2, 1), :]),
-            (1, xt.at[h, r, 0]),
-            (3, xt.at[h, r, 1]),
-        )[m]
-        return remote(src, xr.at[h, r, m], s_x.at[h, r, m], r_x.at[h, r, m], grp_0=lax.rem(x + to, nx))
-
-    def first_x(h, r):
+
+    def block(owner):
+        return pl.ds(pl.multiple_of(lax.rem(owner, nx) * mrow, mrow), mrow)
+
+    def along_x(h, r, k):
+        return remote(
+            xs.at[h, r, block(x + k), :], xr.at[h, r, k], s_x.at[h, r, k], r_x.at[h, r, k], grp_0=lax.rem(x + k, nx)
+        )
+
+    def over_x(h, r):
         to_core(h, r).wait_recv()
         lg[h, r] = lg[h, r] + crecv[h, r].astype(F32)
         xs[h, r] = lg[h, r].astype(BF16)
-        for m in (1, 3, 0, 2):
-            send(along_x(h, r, m))
-
-    def second_x(h, r):
-        along_x(h, r, 1).wait_recv()
-        xt[h, r, 0] = (lg[h, r, block(x + 1, 0), :] + xr[h, r, 1].astype(F32)).astype(BF16)
-        send(along_x(h, r, 4))
-        along_x(h, r, 3).wait_recv()
-        xt[h, r, 1] = (lg[h, r, block(x + 3, 1), :] + xr[h, r, 3].astype(F32)).astype(BF16)
-        send(along_x(h, r, 5))
+        for k in nearest_last(nx):
+            send(along_x(h, r, k))
 
     def along_y(h, r, k):
         to = lax.rem(y + k, ny)
         return remote(ysend.at[h, r, to], yr.at[h, r, k], s_y.at[h, r, k], r_y.at[h, r, k], grp_1=to)
 
     def over_y(h, r):
-        for m in (2, 4, 0, 5):
-            along_x(h, r, m).wait_recv()
-        ymine[h, r, :quarter, :] = lg[h, r, block(x, 0), :] + xr[h, r, 2].astype(F32) + xr[h, r, 4].astype(F32)
-        ymine[h, r, quarter:, :] = lg[h, r, block(x, 1), :] + xr[h, r, 0].astype(F32) + xr[h, r, 5].astype(F32)
+        total = lg[h, r, block(x), :]
+        for k in range(1, nx):
+            along_x(h, r, k).wait_recv()
+            total += xr[h, r, k].astype(F32)
+        ymine[h, r] = total
         ysend[h, r] = ymine[h, r].reshape(ny, piece, half).astype(BF16)
         for k in yring:
             send(along_y(h, r, k))
 
     parts = 2 * (rel + 1)
-    held = -(-parts // nz)
-
-    def along_z(q):
-        k = lax.rem(q - z + 2 * nz, nz)
-        return remote(zsend.at[q], zrecv.at[q // nz, k], s_z.at[q], r_z.at[q // nz, k], dom=q % nz)
+    held = -(-parts // GROUP)
+    owners = nz // GROUP
+
+    def piece_of(h, r):
+        return h if r == rel else 2 + h * rel + r
+
+    def along_z(q, j):
+        owner = q % GROUP + j * GROUP
+        k = lax.rem(owner - z + 2 * nz, nz)
+        return remote(zsend.at[q], zrecv.at[q // GROUP, k], s_z.at[q, j], r_z.at[q // GROUP, k], dom=owner)
 
     def over_z(h, r):
-        q = 2 * r + h
+        q = piece_of(h, r)
         total = ymine[h, r, pl.ds(pl.multiple_of(y * piece, piece), piece), :]
         for k in yring:
             along_y(h, r, k).wait_recv()
             total += yr[h, r, k].astype(F32)
-        zsend[q] = total
-
-        @pl.when(z != q % nz)
+        zmine[q] = total
+        zsend[q] = total.astype(BF16)
+        for j in range(owners):
+            @pl.when(z != q % GROUP + j * GROUP)
+            def _():
+                along_z(q, j).start()
+
+    def shared(i, k):
+        q = lax.rem(z, GROUP) + i * GROUP
+        return remote(zown.at[i], wrecv.at[q], s_w.at[i, k], r_w.at[q], dom=zp(k))
+
+    near = (2, nz - 1, 1)
+
+    def total_z(i):
+        q = lax.rem(z, GROUP) + i * GROUP
+
+        @pl.when(q < parts)
         def _():
-            along_z(q).start()
+            total = zmine[q]
+            for k in range(1, nz):
+                remote(zsend.at[0], zrecv.at[i, k], s_z.at[0, 0], r_z.at[i, k], dom=zp(1)).wait_recv()
+                total += zrecv[i, k].astype(F32)
+            zown[i] = total
+            for k in near:
+                shared(i, k).start()
+            wrecv[q] = total
 
     def units(h):
         return [(h, r) for r in range(rel)]
@@ -255,27 +280,25 @@
     for u in first:
         local(*u)
     for u in first:
-        first_x(*u)
+        over_x(*u)
 
     for k in ring:
         gpull(0, k).wait_recv()
+        gpull(1, k).wait_recv()
     for u in units(0):
         local(*u)
     for u in units(0):
-        first_x(*u)
+        over_x(*u)
     for u in first:
-        second_x(*u)
-
-    for k in ring:
-        gpull(1, k).wait_recv()
+        over_y(*u)
+
+    for k in ring:
+        gpull(2, k).wait_recv()
+        gpull(3, k).wait_recv()
     for u in units(1):
         local(*u)
     for u in units(1):
-        first_x(*u)
-    for u in first:
-        over_y(*u)
-    for u in units(0):
-        second_x(*u)
+        over_x(*u)
 
     for h in (0, 1):
         back[:, h * half : (h + 1) * half] = dot(adj_t[...], gtab[h]).astype(BF16)
@@ -293,8 +316,6 @@
 
     for u in units(0):
         over_y(*u)
-    for u in units(1):
-        second_x(*u)
     for u in first:
         over_z(*u)
 
@@ -307,50 +328,38 @@
         over_y(*u)
     for u in units(0):
         over_z(*u)
+    for u in units(1):
+        over_z(*u)
+    total_z(0)
 
     for k in ring:
         bpush(k).wait_recv()
     ingrad_ref[0] = (bown[...] + dot(place[...], brecv[...].reshape(mirrors, width))).astype(BF16)
 
-    for u in units(1):
-        over_z(*u)
-
-    def shared(i, k):
-        q = z + i * nz
-        return remote(zown.at[i], wrecv.at[q], s_w.at[i, k], r_w.at[q], dom=zp(k))
-
-    for i in range(held):
-        q = z + i * nz
-
-        @pl.when(q < parts)
-        def _():
-            total = zsend[q]
-            for k in range(1, nz):
-                remote(zsend.at[0], zrecv.at[i, k], s_z.at[0], r_z.at[i, k], dom=zp(1)).wait_recv()
-                total += zrecv[i, k]
-            zown[i] = total
-            for k in ring:
-                shared(i, k).start()
-            wrecv[q] = total
-
-    for q in range(parts):
-        @pl.when(z != q % nz)
-        def _():
-            remote(zown.at[0], wrecv.at[q], s_w.at[0, 0], r_w.at[q], dom=zp(1)).wait_recv()
-
-        h = q % 2
-        wgrad_ref[q // 2, :, h * half : (h + 1) * half] = wrecv[q]
+    for i in range(1, held):
+        total_z(i)
+
+    for h in (0, 1):
+        for r in range(rel + 1):
+            q = piece_of(h, r)
+
+            @pl.when(lax.rem(z, GROUP) != q % GROUP)
+            def _():
+                remote(zown.at[0], wrecv.at[q], s_w.at[0, 1], r_w.at[q], dom=zp(1)).wait_recv()
+
+            wgrad_ref[r, :, h * half : (h + 1) * half] = wrecv[q]
 
     for copy in sent:
         copy.wait_send()
     for q in range(parts):
-        @pl.when(z != q % nz)
+        for j in range(owners):
+            @pl.when(z != q % GROUP + j * GROUP)
+            def _():
+                along_z(q, j).wait_send()
+    for i in range(held):
+        @pl.when(lax.rem(z, GROUP) + i * GROUP < parts)
         def _():
-            along_z(q).wait_send()
-    for i in range(held):
-        @pl.when(z + i * nz < parts)
-        def _():
-            for k in ring:
+            for k in near:
                 shared(i, k).wait_send()
 
 
@@ -373,10 +382,12 @@
     rows = mast + mirrors
     edges = edge_source.shape[1]
     half = width // 2
-    mrow = half // 4
-    piece = width // (4 * ny * 2)
+    slab = width // 4
+    nx = NX
+    mrow = half // nx
+    piece = width // (nx * ny * 2)
     parts = 2 * (rel + 1)
-    held = -(-parts // nz)
+    held = -(-parts // GROUP)
     vmem = pl.BlockSpec(memory_space=pltpu.VMEM)
     hbm = pl.BlockSpec(memory_space=pl.ANY)
     dma = pltpu.SemaphoreType.DMA
@@ -398,10 +409,10 @@
         pltpu.VMEM((rel * rows, width), BF16),
         pltpu.VMEM((rel + 1, 2, half, rows), BF16),
         pltpu.VMEM((nz, cap, width), BF16),
-        pltpu.VMEM((2, nz, cap, half), BF16),
-        pltpu.VMEM((2, nz, cap, half), BF16),
-        pltpu.VMEM((2, mast, half), F32),
-        pltpu.VMEM((2, nz, cap, half), BF16),
+        pltpu.VMEM((4, nz, cap, slab), BF16),
+        pltpu.VMEM((4, nz, cap, slab), BF16),
+        pltpu.VMEM((4, mast, slab), F32),
+        pltpu.VMEM((4, nz, cap, slab), BF16),
         pltpu.VMEM((2, rows, half), BF16),
         pltpu.VMEM((rel * rows, width), BF16),
         pltpu.VMEM((mast, width), F32),
@@ -411,24 +422,24 @@
         pltpu.VMEM((2, rel + 1, half, half), BF16),
         pltpu.VMEM((2, rel + 1, half, half), F32),
         pltpu.VMEM((2, rel + 1, half, half), BF16),
-        pltpu.VMEM((2, rel + 1, 6, mrow // 2, half), BF16),
-        pltpu.VMEM((2, rel + 1, 2, mrow // 2, half), BF16),
+        pltpu.VMEM((2, rel + 1, nx, mrow, half), BF16),
         pltpu.VMEM((2, rel + 1, ny, piece, half), BF16),
         pltpu.VMEM((2, rel + 1, mrow, half), F32),
         pltpu.VMEM((2, rel + 1, ny, piece, half), BF16),
         pltpu.VMEM((parts, piece, half), F32),
-        pltpu.VMEM((held, nz, piece, half), F32),
+        pltpu.VMEM((parts, piece, half), BF16),
+        pltpu.VMEM((held, nz, piece, half), BF16),
         pltpu.VMEM((held, piece, half), F32),
         pltpu.VMEM((parts, piece, half), F32),
         dma((9,)),
         dma((nz,)), dma((nz,)),
-        dma((2, nz)), dma((2, nz)),
-        dma((2, nz)), dma((2, nz)),
+        dma((4, nz)), dma((4, nz)),
+        dma((4, nz)), dma((4, nz)),
         dma((nz,)), dma((nz,)),
         dma((2, rel + 1)), dma((2, rel + 1)),
-        dma((2, rel + 1, 6)), dma((2, rel + 1, 6)),
+        dma((2, rel + 1, nx)), dma((2, rel + 1, nx)),
         dma((2, rel + 1, ny)), dma((2, rel + 1, ny)),
-        dma((parts,)), dma((held, nz)),
+        dma((parts, nz // GROUP)), dma((held, nz)),
         dma((held, nz)), dma((parts,)),
     ]
     out_shape = (
@@ -463,7 +474,7 @@
 def solution(mesh):
     devices = mesh.devices.shape[1]
     finer = Mesh(
-        mesh.devices.reshape(mesh.shape["dom"], 4, devices // 8, 2), ("dom", "grp_0", "grp_1", "grp_2")
+        mesh.devices.reshape(mesh.shape["dom"], NX, devices // (2 * NX), 2), ("dom", "grp_0", "grp_1", "grp_2")
     )
     in_specs = (
         P(GRP, "dom", None),

time: 81.5 us -> 77.9 us (0.956)
  the two profiles are of different devices: /device:TPU:8 before, /device:TPU:1 now
where the time goes in v2:
time: 77.9 us; the launch traced here: 76.6 us
  Pallas kernels  76 us (98%)
    pallas_call x1, Pallas kernels, per_device(): pl.pallas_call(functools.partial(kernel, nz, ny, cap), out_shape=tuple((p...  75.2 us

profile of v2, /device:TPU:1, one launch (start us, length us, event | category | flops | bytes accessed | tf_op | source)
XLA Modules:
  0.0 76.6 jit_solution(17487817034038751521)
XLA Ops:
  0.6 75.2 %graph_conv_step.1 = (bf16[1,128,512]{2,1,0:T(8,128)(2,1)S(1)}, bf16[1,128,512]{2,1,0:T(8,128)(2,1)S(1)}, f32[5,8,512]{2,1,0:T(8,128)S(1)}) custom-call(s32[1,12]{1,0:T(1,128)} %counts_hbm.1, bf16[1,128,512]{2,1,0:T(8,128)(2,1)} %masters_hbm.1, bf16[1,128,512]{2,1,0:T(8,128)(2,1)} %cotan_hbm.1, s32[1,2048]{1,0:T(1,128)} %source_hbm.1, s32[1,2048]{1,0:T(1,128)} %target_hbm.1, ...), custom_call_target="tpu_custom_call" | custom-call | tf_op jit(solution)/shard_map/graph_conv_step/pallas_call | solution.py:450
  75.9 0.7 handed_on.1

commit v3 on v2

--- a/solution.py
+++ b/solution.py
@@ -33,10 +33,10 @@
     counts_hbm, masters_hbm, cotan_hbm, source_hbm, target_hbm, relation_hbm, slots_hbm, relw_hbm, selfw_hbm,
     act_ref, ingrad_ref, wgrad_ref,
     counts, cotan, source, target, relation, slots, relw, selfw, one_hot, adj, adj_t, place, pick, table, agg, agg_t,
-    psend, qsend, qrecv, own, gsend, gtab, back, bown, bsend, brecv, csend, crecv, lg, xs, xr, ysend, ymine, yr,
-    zmine, zsend, zrecv, zown, wrecv,
+    psend, qsend, qrecv, own, gsend, gtab, back, bown, bsend, brecv, self_t, pagg, pself, pgt, lg, xs, xr, ysend, ymine, yr,
+    fs, fyr, fmine, fxs, fxr, zmine, zsend, zrecv, zown, wrecv,
     in_sem, s_pull, r_pull, s_push, r_push, s_gpull, r_gpull, s_back, r_back, s_core, r_core, s_x, r_x, s_y, r_y,
-    s_z, r_z, s_w, r_w,
+    s_fy, r_fy, s_fx, r_fx, s_z, r_z, s_w, r_w,
 ):
     z = lax.axis_index("dom")
     x = lax.axis_index("grp_0")
@@ -165,7 +165,21 @@
         for core, values in enumerate(transposed(agg[r * rows : (r + 1) * rows, :])):
             agg_t[r, core] = values
     for core, values in enumerate(transposed(table[:mast, :])):
-        agg_t[rel, core, :, :mast] = values
+        self_t[core] = values
+
+    def to_core(src, dst, n):
+        return remote(src, dst, s_core.at[n], r_core.at[n], grp_2=1 - c)
+
+    give_agg = to_core(agg_t.at[:, 1 - c], pagg, 0)
+    give_self = to_core(self_t.at[1 - c], pself, 1)
+    send(give_agg)
+    send(give_self)
+
+    def give_masters(h):
+        return to_core(gtab.at[h, :mast, :], pgt.at[h, :mast, :], 2 + h)
+
+    def give_mirrors(h):
+        return to_core(gtab.at[h, mast:, :], pgt.at[h, mast:, :], 4 + h)
 
     counted(adj_t, source[...], target[...])
 
@@ -187,15 +201,10 @@
         gtab[b // 2, :mast, part_cols] = grad
         gtab[b // 2, mirror_rows(), part_cols] = gsend[b, z]
         act_ref[0, :, cols] = (value * gate).astype(BF16)
-
-    def to_core(h, r):
-        return remote(csend.at[h, r], crecv.at[h, r], s_core.at[h, r], r_core.at[h, r], grp_2=1 - c)
-
-    def local(h, r):
-        seen = mast if r == rel else rows
-        csend[h, r] = dot(agg_t[r, 1 - c, :, :seen], gtab[h, :seen, :]).astype(BF16)
-        send(to_core(h, r))
-        lg[h, r] = dot(agg_t[r, c, :, :seen], gtab[h, :seen, :])
+        if b % 2:
+            send(give_masters(b // 2))
+
+    swapped = rel - 1
 
     mrow = half // nx
 
@@ -208,11 +217,34 @@
         )
 
     def over_x(h, r):
-        to_core(h, r).wait_recv()
-        lg[h, r] = lg[h, r] + crecv[h, r].astype(F32)
         xs[h, r] = lg[h, r].astype(BF16)
         for k in nearest_last(nx):
             send(along_x(h, r, k))
+
+    def along_y_first(h, k):
+        to = lax.rem(y + k, ny)
+        return remote(fs.at[h, :, to], fyr.at[h, k], s_fy.at[h, k], r_fy.at[h, k], grp_1=to)
+
+    def over_y_first(h):
+        fs[h] = lg[h, swapped].reshape(nx, ny, piece, half).astype(BF16)
+        for k in yring:
+            send(along_y_first(h, k))
+
+    def along_x_last(h, k):
+        to = lax.rem(x + k, nx)
+        return remote(fxs.at[h, to], fxr.at[h, k], s_fx.at[h, k], r_fx.at[h, k], grp_0=to)
+
+    def over_x_last(h):
+        for k in yring:
+            along_y_first(h, k).wait_recv()
+        for owner in range(nx):
+            total = lg[h, swapped, pl.ds(pl.multiple_of((owner * ny + y) * piece, piece), piece), :]
+            for k in yring:
+                total += fyr[h, k, owner].astype(F32)
+            fmine[h, owner] = total
+            fxs[h, owner] = total.astype(BF16)
+        for k in nearest_last(nx):
+            send(along_x_last(h, k))
 
     def along_y(h, r, k):
         to = lax.rem(y + k, ny)
@@ -242,10 +274,16 @@
 
     def over_z(h, r):
         q = piece_of(h, r)
-        total = ymine[h, r, pl.ds(pl.multiple_of(y * piece, piece), piece), :]
-        for k in yring:
-            along_y(h, r, k).wait_recv()
-            total += yr[h, r, k].astype(F32)
+        if r == swapped:
+            total = fmine[h, x]
+            for k in range(1, nx):
+                along_x_last(h, k).wait_recv()
+                total += fxr[h, k].astype(F32)
+        else:
+            total = ymine[h, r, pl.ds(pl.multiple_of(y * piece, piece), piece), :]
+            for k in yring:
+                along_y(h, r, k).wait_recv()
+                total += yr[h, r, k].astype(F32)
         zmine[q] = total
         zsend[q] = total.astype(BF16)
         for j in range(owners):
@@ -274,31 +312,34 @@
             wrecv[q] = total
 
     def units(h):
-        return [(h, r) for r in range(rel)]
+        return [(h, r) for r in range(rel) if r != swapped]
 
     first = [(0, rel), (1, rel)]
-    for u in first:
-        local(*u)
-    for u in first:
-        over_x(*u)
-
-    for k in ring:
-        gpull(0, k).wait_recv()
-        gpull(1, k).wait_recv()
-    for u in units(0):
-        local(*u)
-    for u in units(0):
-        over_x(*u)
-    for u in first:
-        over_y(*u)
-
-    for k in ring:
-        gpull(2, k).wait_recv()
-        gpull(3, k).wait_recv()
-    for u in units(1):
-        local(*u)
-    for u in units(1):
-        over_x(*u)
+    give_agg.wait_recv()
+    give_self.wait_recv()
+    for h in (0, 1):
+        give_masters(h).wait_recv()
+        lg[h, rel] = dot(self_t[c], gtab[h, :mast, :]) + dot(pself[...], pgt[h, :mast, :])
+        over_x(h, rel)
+
+    for h in (0, 1):
+        for k in ring:
+            gpull(2 * h, k).wait_recv()
+            gpull(2 * h + 1, k).wait_recv()
+        send(give_mirrors(h))
+        order = [swapped] + list(range(swapped))
+        for r in order:
+            lg[h, r] = dot(agg_t[r, c], gtab[h])
+        give_mirrors(h).wait_recv()
+        for r in order:
+            lg[h, r] = lg[h, r] + dot(pagg[r], pgt[h])
+            if r == swapped:
+                over_y_first(h)
+            else:
+                over_x(h, r)
+        if h == 0:
+            for u in first:
+                over_y(*u)
 
     for h in (0, 1):
         back[:, h * half : (h + 1) * half] = dot(adj_t[...], gtab[h]).astype(BF16)
@@ -318,6 +359,7 @@
         over_y(*u)
     for u in first:
         over_z(*u)
+    over_x_last(0)
 
     part = dot_nt(gtab[0, :mast, :], selfw[:, :half]) + dot_nt(gtab[1, :mast, :], selfw[:, half:])
     for r in range(rel):
@@ -328,8 +370,11 @@
         over_y(*u)
     for u in units(0):
         over_z(*u)
+    over_z(0, swapped)
+    over_x_last(1)
     for u in units(1):
         over_z(*u)
+    over_z(1, swapped)
     total_z(0)
 
     for k in ring:
@@ -407,7 +452,7 @@
         pltpu.VMEM((mirrors, mast), BF16),
         pltpu.VMEM((rows, width), BF16),
         pltpu.VMEM((rel * rows, width), BF16),
-        pltpu.VMEM((rel + 1, 2, half, rows), BF16),
+        pltpu.VMEM((rel, 2, half, rows), BF16),
         pltpu.VMEM((nz, cap, width), BF16),
         pltpu.VMEM((4, nz, cap, slab), BF16),
         pltpu.VMEM((4, nz, cap, slab), BF16),
@@ -418,14 +463,21 @@
         pltpu.VMEM((mast, width), F32),
         pltpu.VMEM((nz, cap, width), BF16),
         pltpu.VMEM((nz, cap, width), BF16),
-        pltpu.VMEM((2, rel + 1, half, half), BF16),
-        pltpu.VMEM((2, rel + 1, half, half), BF16),
+        pltpu.VMEM((2, half, mast), BF16),
+        pltpu.VMEM((rel, half, rows), BF16),
+        pltpu.VMEM((half, mast), BF16),
+        pltpu.VMEM((2, rows, half), BF16),
         pltpu.VMEM((2, rel + 1, half, half), F32),
         pltpu.VMEM((2, rel + 1, half, half), BF16),
         pltpu.VMEM((2, rel + 1, nx, mrow, half), BF16),
         pltpu.VMEM((2, rel + 1, ny, piece, half), BF16),
         pltpu.VMEM((2, rel + 1, mrow, half), F32),
         pltpu.VMEM((2, rel + 1, ny, piece, half), BF16),
+        pltpu.VMEM((2, nx, ny, piece, half), BF16),
+        pltpu.VMEM((2, ny, nx, piece, half), BF16),
+        pltpu.VMEM((2, nx, piece, half), F32),
+        pltpu.VMEM((2, nx, piece, half), BF16),
+        pltpu.VMEM((2, nx, piece, half), BF16),
         pltpu.VMEM((parts, piece, half), F32),
         pltpu.VMEM((parts, piece, half), BF16),
         pltpu.VMEM((held, nz, piece, half), BF16),
@@ -436,9 +488,11 @@
         dma((4, nz)), dma((4, nz)),
         dma((4, nz)), dma((4, nz)),
         dma((nz,)), dma((nz,)),
-        dma((2, rel + 1)), dma((2, rel + 1)),
+        dma((6,)), dma((6,)),
         dma((2, rel + 1, nx)), dma((2, rel + 1, nx)),
         dma((2, rel + 1, ny)), dma((2, rel + 1, ny)),
+        dma((2, ny)), dma((2, ny)),
+        dma((2, nx)), dma((2, nx)),
         dma((parts, nz // GROUP)), dma((held, nz)),
         dma((held, nz)), dma((parts,)),
     ]

time: 77.9 us -> 75.7 us (0.972); the launches traced: 76.6 us -> 75.5 us
  Pallas kernels: 76 us -> 74.9 us
    pallas_call x1, Pallas kernels: 75.2 us -> 74.1 us  [per_device(): pl.pallas_call(functools.partial(kernel, nz, ny, cap), out_shape=tuple((p...]
where the time goes in v3:
time: 75.7 us; the launch traced here: 75.5 us
  Pallas kernels  74.9 us (99%)
    pallas_call x1, Pallas kernels, per_device(): pl.pallas_call(functools.partial(kernel, nz, ny, cap), out_shape=tuple((p...  74.1 us

profile of v3, /device:TPU:1, one launch (start us, length us, event | category | flops | bytes accessed | tf_op | source)
XLA Modules:
  0.0 75.5 jit_solution(12565762435601413863)
XLA Ops:
  0.6 74.1 %graph_conv_step.1 = (bf16[1,128,512]{2,1,0:T(8,128)(2,1)S(1)}, bf16[1,128,512]{2,1,0:T(8,128)(2,1)S(1)}, f32[5,8,512]{2,1,0:T(8,128)S(1)}) custom-call(s32[1,12]{1,0:T(1,128)} %counts_hbm.1, bf16[1,128,512]{2,1,0:T(8,128)(2,1)} %masters_hbm.1, bf16[1,128,512]{2,1,0:T(8,128)(2,1)} %cotan_hbm.1, s32[1,2048]{1,0:T(1,128)} %source_hbm.1, s32[1,2048]{1,0:T(1,128)} %target_hbm.1, ...), custom_call_target="tpu_custom_call" | custom-call | tf_op jit(solution)/shard_map/graph_conv_step/pallas_call | solution.py:504
  74.8 0.7 handed_on.1

commit v4 on v3

--- a/solution.py
+++ b/solution.py
@@ -33,9 +33,9 @@
     counts_hbm, masters_hbm, cotan_hbm, source_hbm, target_hbm, relation_hbm, slots_hbm, relw_hbm, selfw_hbm,
     act_ref, ingrad_ref, wgrad_ref,
     counts, cotan, source, target, relation, slots, relw, selfw, one_hot, adj, adj_t, place, pick, table, agg, agg_t,
-    psend, qsend, qrecv, own, gsend, gtab, back, bown, bsend, brecv, self_t, pagg, pself, pgt, lg, xs, xr, ysend, ymine, yr,
-    fs, fyr, fmine, fxs, fxr, zmine, zsend, zrecv, zown, wrecv,
-    in_sem, s_pull, r_pull, s_push, r_push, s_gpull, r_gpull, s_back, r_back, s_core, r_core, s_x, r_x, s_y, r_y,
+    psend, qsend, qrecv, own, gsend, gtab, back, bown, bsend, brecv, self_t, pagg, pself, pgt, s_arrays, w_arrays,
+    flg, fs, fyr, fmine, fxs, fxr, zmine, zsend, zrecv, zown, wrecv,
+    in_sem, s_pull, r_pull, s_push, r_push, s_gpull, r_gpull, s_back, r_back, s_core, r_core,
     s_fy, r_fy, s_fx, r_fx, s_z, r_z, s_w, r_w,
 ):
     z = lax.axis_index("dom")
@@ -178,8 +178,12 @@
     def give_masters(h):
         return to_core(gtab.at[h, :mast, :], pgt.at[h, :mast, :], 2 + h)
 
-    def give_mirrors(h):
-        return to_core(gtab.at[h, mast:, :], pgt.at[h, mast:, :], 4 + h)
+    def slab_of(b):
+        return slice((b % 2) * slab, (b % 2 + 1) * slab)
+
+    def give_mirrors(b):
+        some = (b // 2, slice(mast, rows), slab_of(b))
+        return to_core(gtab.at[some], pgt.at[some], 4 + b)
 
     counted(adj_t, source[...], target[...])
 
@@ -211,22 +215,23 @@
     def block(owner):
         return pl.ds(pl.multiple_of(lax.rem(owner, nx) * mrow, mrow), mrow)
 
-    def along_x(h, r, k):
-        return remote(
-            xs.at[h, r, block(x + k), :], xr.at[h, r, k], s_x.at[h, r, k], r_x.at[h, r, k], grp_0=lax.rem(x + k, nx)
-        )
-
-    def over_x(h, r):
-        xs[h, r] = lg[h, r].astype(BF16)
+    def along_x(group, i, k):
+        lg, xs, xr, ysend, ymine, yr, s_x, r_x, s_y, r_y = group
+        to = lax.rem(x + k, nx)
+        return remote(xs.at[i, :, block(x + k), :], xr.at[i, k], s_x.at[i, k], r_x.at[i, k], grp_0=to)
+
+    def over_x(group, i):
+        lg, xs = group[:2]
+        xs[i] = lg[i].astype(BF16)
         for k in nearest_last(nx):
-            send(along_x(h, r, k))
+            send(along_x(group, i, k))
 
     def along_y_first(h, k):
         to = lax.rem(y + k, ny)
         return remote(fs.at[h, :, to], fyr.at[h, k], s_fy.at[h, k], r_fy.at[h, k], grp_1=to)
 
     def over_y_first(h):
-        fs[h] = lg[h, swapped].reshape(nx, ny, piece, half).astype(BF16)
+        fs[h] = flg[h].reshape(nx, ny, piece, slab).astype(BF16)
         for k in yring:
             send(along_y_first(h, k))
 
@@ -238,7 +243,7 @@
         for k in yring:
             along_y_first(h, k).wait_recv()
         for owner in range(nx):
-            total = lg[h, swapped, pl.ds(pl.multiple_of((owner * ny + y) * piece, piece), piece), :]
+            total = flg[h, pl.ds(pl.multiple_of((owner * ny + y) * piece, piece), piece), :]
             for k in yring:
                 total += fyr[h, k, owner].astype(F32)
             fmine[h, owner] = total
@@ -246,46 +251,56 @@
         for k in nearest_last(nx):
             send(along_x_last(h, k))
 
-    def along_y(h, r, k):
+    def along_y(group, i, k):
+        lg, xs, xr, ysend, ymine, yr, s_x, r_x, s_y, r_y = group
         to = lax.rem(y + k, ny)
-        return remote(ysend.at[h, r, to], yr.at[h, r, k], s_y.at[h, r, k], r_y.at[h, r, k], grp_1=to)
-
-    def over_y(h, r):
-        total = lg[h, r, block(x), :]
+        return remote(ysend.at[i, :, to], yr.at[i, k], s_y.at[i, k], r_y.at[i, k], grp_1=to)
+
+    def over_y(group, i):
+        lg, xs, xr, ysend, ymine = group[:5]
         for k in range(1, nx):
-            along_x(h, r, k).wait_recv()
-            total += xr[h, r, k].astype(F32)
-        ymine[h, r] = total
-        ysend[h, r] = ymine[h, r].reshape(ny, piece, half).astype(BF16)
+            along_x(group, i, k).wait_recv()
+        for n in range(lg.shape[1]):
+            total = lg[i, n, block(x), :]
+            for k in range(1, nx):
+                total += xr[i, k, n].astype(F32)
+            ymine[i, n] = total
+            ysend[i, n] = total.reshape(ny, piece, total.shape[1]).astype(BF16)
         for k in yring:
-            send(along_y(h, r, k))
-
-    parts = 2 * (rel + 1)
+            send(along_y(group, i, k))
+
+    def from_y(group, i):
+        ymine, yr = group[4:6]
+        for k in yring:
+            along_y(group, i, k).wait_recv()
+        totals = []
+        for n in range(ymine.shape[1]):
+            total = ymine[i, n, pl.ds(pl.multiple_of(y * piece, piece), piece), :]
+            for k in yring:
+                total += yr[i, k, n].astype(F32)
+            totals.append(total)
+        return totals
+
+    def from_x(b):
+        total = fmine[b, x]
+        for k in range(1, nx):
+            along_x_last(b, k).wait_recv()
+            total += fxr[b, k].astype(F32)
+        return total
+
+    parts = 5
     held = -(-parts // GROUP)
     owners = nz // GROUP
-
-    def piece_of(h, r):
-        return h if r == rel else 2 + h * rel + r
 
     def along_z(q, j):
         owner = q % GROUP + j * GROUP
         k = lax.rem(owner - z + 2 * nz, nz)
         return remote(zsend.at[q], zrecv.at[q // GROUP, k], s_z.at[q, j], r_z.at[q // GROUP, k], dom=owner)
 
-    def over_z(h, r):
-        q = piece_of(h, r)
-        if r == swapped:
-            total = fmine[h, x]
-            for k in range(1, nx):
-                along_x_last(h, k).wait_recv()
-                total += fxr[h, k].astype(F32)
-        else:
-            total = ymine[h, r, pl.ds(pl.multiple_of(y * piece, piece), piece), :]
-            for k in yring:
-                along_y(h, r, k).wait_recv()
-                total += yr[h, r, k].astype(F32)
-        zmine[q] = total
-        zsend[q] = total.astype(BF16)
+    def over_z(q, slabs):
+        for n, total in enumerate(slabs):
+            zmine[q, n] = total
+            zsend[q, n] = total.astype(BF16)
         for j in range(owners):
             @pl.when(z != q % GROUP + j * GROUP)
             def _():
@@ -311,35 +326,31 @@
                 shared(i, k).start()
             wrecv[q] = total
 
-    def units(h):
-        return [(h, r) for r in range(rel) if r != swapped]
-
-    first = [(0, rel), (1, rel)]
     give_agg.wait_recv()
     give_self.wait_recv()
     for h in (0, 1):
         give_masters(h).wait_recv()
-        lg[h, rel] = dot(self_t[c], gtab[h, :mast, :]) + dot(pself[...], pgt[h, :mast, :])
-        over_x(h, rel)
-
-    for h in (0, 1):
+        s_arrays[0][h, 0] = dot(self_t[c], gtab[h, :mast, :]) + dot(pself[...], pgt[h, :mast, :])
+        over_x(s_arrays, h)
+
+    wlg = w_arrays[0]
+    for b in range(4):
         for k in ring:
-            gpull(2 * h, k).wait_recv()
-            gpull(2 * h + 1, k).wait_recv()
-        send(give_mirrors(h))
-        order = [swapped] + list(range(swapped))
-        for r in order:
-            lg[h, r] = dot(agg_t[r, c], gtab[h])
-        give_mirrors(h).wait_recv()
-        for r in order:
-            lg[h, r] = lg[h, r] + dot(pagg[r], pgt[h])
-            if r == swapped:
-                over_y_first(h)
-            else:
-                over_x(h, r)
-        if h == 0:
-            for u in first:
-                over_y(*u)
+            gpull(b, k).wait_recv()
+        send(give_mirrors(b))
+        flg[b] = dot(agg_t[swapped, c], gtab[b // 2, :, slab_of(b)])
+        for r in range(swapped):
+            wlg[b, r] = dot(agg_t[r, c], gtab[b // 2, :, slab_of(b)])
+        give_mirrors(b).wait_recv()
+        flg[b] = flg[b] + dot(pagg[swapped], pgt[b // 2, :, slab_of(b)])
+        over_y_first(b)
+        for r in range(swapped):
+            wlg[b, r] = wlg[b, r] + dot(pagg[r], pgt[b // 2, :, slab_of(b)])
+        over_x(w_arrays, b)
+        if b == 1:
+            over_y(s_arrays, 0)
+            over_y(s_arrays, 1)
+    over_y(w_arrays, 0)
 
     for h in (0, 1):
         back[:, h * half : (h + 1) * half] = dot(adj_t[...], gtab[h]).astype(BF16)
@@ -355,26 +366,22 @@
     for k in ring:
         send(bpush(k))
 
-    for u in units(0):
-        over_y(*u)
-    for u in first:
-        over_z(*u)
+    over_y(w_arrays, 1)
     over_x_last(0)
+    over_y(w_arrays, 2)
+    over_x_last(1)
 
     part = dot_nt(gtab[0, :mast, :], selfw[:, :half]) + dot_nt(gtab[1, :mast, :], selfw[:, half:])
     for r in range(rel):
         part += dot_nt(back[r * rows : r * rows + mast, :], relw[r])
     bown[...] = part
 
-    for u in units(1):
-        over_y(*u)
-    for u in units(0):
-        over_z(*u)
-    over_z(0, swapped)
-    over_x_last(1)
-    for u in units(1):
-        over_z(*u)
-    over_z(1, swapped)
+    over_y(w_arrays, 3)
+    over_z(0, [t[:, i * slab : (i + 1) * slab] for h in (0, 1) for t in from_y(s_arrays, h) for i in (0, 1)])
+    over_x_last(2)
+    over_x_last(3)
+    for b in range(4):
+        over_z(1 + b, from_y(w_arrays, b) + [from_x(b)])
     total_z(0)
 
     for k in ring:
@@ -384,15 +391,14 @@
     for i in range(1, held):
         total_z(i)
 
-    for h in (0, 1):
-        for r in range(rel + 1):
-            q = piece_of(h, r)
-
-            @pl.when(lax.rem(z, GROUP) != q % GROUP)
-            def _():
-                remote(zown.at[0], wrecv.at[q], s_w.at[0, 1], r_w.at[q], dom=zp(1)).wait_recv()
-
-            wgrad_ref[r, :, h * half : (h + 1) * half] = wrecv[q]
+    for q in range(parts):
+        @pl.when(lax.rem(z, GROUP) != q % GROUP)
+        def _():
+            remote(zown.at[0], wrecv.at[q], s_w.at[0, 1], r_w.at[q], dom=zp(1)).wait_recv()
+
+        for n in range(4):
+            r, b = (n, q - 1) if q else (rel, n)
+            wgrad_ref[r, :, b * slab : (b + 1) * slab] = wrecv[q, n]
 
     for copy in sent:
         copy.wait_send()
@@ -431,11 +437,24 @@
     nx = NX
     mrow = half // nx
     piece = width // (nx * ny * 2)
-    parts = 2 * (rel + 1)
+    parts = 5
     held = -(-parts // GROUP)
     vmem = pl.BlockSpec(memory_space=pltpu.VMEM)
     hbm = pl.BlockSpec(memory_space=pl.ANY)
     dma = pltpu.SemaphoreType.DMA
+
+    def summed(units, many, columns):
+        return (
+            pltpu.VMEM((units, many, half, columns), F32),
+            pltpu.VMEM((units, many, half, columns), BF16),
+            pltpu.VMEM((units, nx, many, mrow, columns), BF16),
+            pltpu.VMEM((units, many, ny, piece, columns), BF16),
+            pltpu.VMEM((units, many, mrow, columns), F32),
+            pltpu.VMEM((units, ny, many, piece, columns), BF16),
+            dma((units, nx)), dma((units, nx)),
+            dma((units, ny)), dma((units, ny)),
+        )
+
     scratch = [
         pltpu.SMEM((1, nz), jnp.int32),
         pltpu.VMEM((mast, width), BF16),
@@ -467,32 +486,27 @@
         pltpu.VMEM((rel, half, rows), BF16),
         pltpu.VMEM((half, mast), BF16),
         pltpu.VMEM((2, rows, half), BF16),
-        pltpu.VMEM((2, rel + 1, half, half), F32),
-        pltpu.VMEM((2, rel + 1, half, half), BF16),
-        pltpu.VMEM((2, rel + 1, nx, mrow, half), BF16),
-        pltpu.VMEM((2, rel + 1, ny, piece, half), BF16),
-        pltpu.VMEM((2, rel + 1, mrow, half), F32),
-        pltpu.VMEM((2, rel + 1, ny, piece, half), BF16),
-        pltpu.VMEM((2, nx, ny, piece, half), BF16),
-        pltpu.VMEM((2, ny, nx, piece, half), BF16),
-        pltpu.VMEM((2, nx, piece, half), F32),
-        pltpu.VMEM((2, nx, piece, half), BF16),
-        pltpu.VMEM((2, nx, piece, half), BF16),
-        pltpu.VMEM((parts, piece, half), F32),
-        pltpu.VMEM((parts, piece, half), BF16),
-        pltpu.VMEM((held, nz, piece, half), BF16),
-        pltpu.VMEM((held, piece, half), F32),
-        pltpu.VMEM((parts, piece, half), F32),
+        summed(2, 1, half),
+        summed(4, rel - 1, slab),
+        pltpu.VMEM((4, half, slab), F32),
+        pltpu.VMEM((4, nx, ny, piece, slab), BF16),
+        pltpu.VMEM((4, ny, nx, piece, slab), BF16),
+        pltpu.VMEM((4, nx, piece, slab), F32),
+        pltpu.VMEM((4, nx, piece, slab), BF16),
+        pltpu.VMEM((4, nx, piece, slab), BF16),
+        pltpu.VMEM((parts, 4, piece, slab), F32),
+        pltpu.VMEM((parts, 4, piece, slab), BF16),
+        pltpu.VMEM((held, nz, 4, piece, slab), BF16),
+        pltpu.VMEM((held, 4, piece, slab), F32),
+        pltpu.VMEM((parts, 4, piece, slab), F32),
         dma((9,)),
         dma((nz,)), dma((nz,)),
         dma((4, nz)), dma((4, nz)),
         dma((4, nz)), dma((4, nz)),
         dma((nz,)), dma((nz,)),
-        dma((6,)), dma((6,)),
-        dma((2, rel + 1, nx)), dma((2, rel + 1, nx)),
-        dma((2, rel + 1, ny)), dma((2, rel + 1, ny)),
-        dma((2, ny)), dma((2, ny)),
-        dma((2, nx)), dma((2, nx)),
+        dma((8,)), dma((8,)),
+        dma((4, ny)), dma((4, ny)),
+        dma((4, nx)), dma((4, nx)),
         dma((parts, nz // GROUP)), dma((held, nz)),
         dma((held, nz)), dma((parts,)),
     ]

time: 75.7 us -> 73.6 us (0.972)
  Pallas kernels: 74.9 us -> 72.5 us
    pallas_call x1, Pallas kernels: 74.1 us -> 71.7 us  [per_device(): pl.pallas_call(functools.partial(kernel, nz, ny, cap), out_shape=tuple((p...]
where the time goes in v4:
time: 73.6 us; the launch traced here: 73.1 us
  Pallas kernels  72.5 us (99%)
    pallas_call x1, Pallas kernels, per_device(): pl.pallas_call(functools.partial(kernel, nz, ny, cap), out_shape=tuple((p...  71.7 us

profile of v4, /device:TPU:1, one launch (start us, length us, event | category | flops | bytes accessed | tf_op | source)
XLA Modules:
  0.0 73.1 jit_solution(14501948389772076777)
XLA Ops:
  0.6 71.7 %graph_conv_step.1 = (bf16[1,128,512]{2,1,0:T(8,128)(2,1)S(1)}, bf16[1,128,512]{2,1,0:T(8,128)(2,1)S(1)}, f32[5,8,512]{2,1,0:T(8,128)S(1)}) custom-call(s32[1,12]{1,0:T(1,128)} %counts_hbm.1, bf16[1,128,512]{2,1,0:T(8,128)(2,1)} %masters_hbm.1, bf16[1,128,512]{2,1,0:T(8,128)(2,1)} %cotan_hbm.1, s32[1,2048]{1,0:T(1,128)} %source_hbm.1, s32[1,2048]{1,0:T(1,128)} %target_hbm.1, ...), custom_call_target="tpu_custom_call" | custom-call | tf_op jit(solution)/shard_map/graph_conv_step/pallas_call | solution.py:518
  72.4 0.7 %handed_on.1 = (bf16[1,128,512]{2,1,0:T(8,128)(2,1)}, bf16[1,128,512]{2,1,0:T(8,128)(2,1)}, f32[5,8,512]{2,1,0:T(8,128)}) custom-call(bf16[1,128,512]{2,1,0:T(8,128)(2,1)S(1)} %get-tuple-element.6.refs_0_, bf16[1,128,512]{2,1,0:T(8,128)(2,1)S(1)} %get-tuple-element.7.refs_1_, f32[5,8,512]{2,1,0:T(8,128)S(1)} %get-tuple-element.8.refs_2_), custom_call_target="tpu_custom_call" | custom-call | tf_op jit(solution)/shard_map/handed_on/pallas_call | solution.py:532

commit v5 on v4

--- a/solution.py
+++ b/solution.py
@@ -22,6 +22,10 @@
 
 def dot_nt(a, b):
     return lax.dot_general(a, b, (((1,), (1,)), ((), ())), preferred_element_type=F32)
+
+
+def transposed_whole(values):
+    return values.astype(F32).T.astype(BF16)
 
 
 def nearest_last(n):
@@ -185,7 +189,8 @@
         some = (b // 2, slice(mast, rows), slab_of(b))
         return to_core(gtab.at[some], pgt.at[some], 4 + b)
 
-    counted(adj_t, source[...], target[...])
+    for r in range(rel):
+        adj_t[r * rows : (r + 1) * rows, :] = transposed_whole(adj[r * rows : (r + 1) * rows, :])
 
     def gpull(b, k):
         at = gtab.at[b // 2, mirror_rows(), pl.ds((b % 2) * slab, slab)]
@@ -354,6 +359,7 @@
 
     for h in (0, 1):
         back[:, h * half : (h + 1) * half] = dot(adj_t[...], gtab[h]).astype(BF16)
+    over_y(w_arrays, 1)
     part = dot_nt(back[mast:rows, :], relw[0])
     for r in range(1, rel):
         part += dot_nt(back[r * rows + mast : (r + 1) * rows, :], relw[r])
@@ -366,7 +372,6 @@
     for k in ring:
         send(bpush(k))
 
-    over_y(w_arrays, 1)
     over_x_last(0)
     over_y(w_arrays, 2)
     over_x_last(1)

time: 73.6 us -> 74.7 us (1.015)
  Pallas kernels: 72.5 us -> 73.9 us
    pallas_call x1, Pallas kernels: 71.7 us -> 73.1 us  [per_device(): pl.pallas_call(functools.partial(kernel, nz, ny, cap), out_shape=tuple((p...]
where the time goes in v5:
time: 74.7 us; the launch traced here: 74.5 us
  Pallas kernels  73.9 us (99%)
    pallas_call x1, Pallas kernels, per_device(): pl.pallas_call(functools.partial(kernel, nz, ny, cap), out_shape=tuple((p...  73.1 us

profile of v5, /device:TPU:1, one launch (start us, length us, event | category | flops | bytes accessed | tf_op | source)
XLA Modules:
  0.0 74.5 jit_solution(16349814456311161645)
XLA Ops:
  0.6 73.1 %graph_conv_step.1 = (bf16[1,128,512]{2,1,0:T(8,128)(2,1)S(1)}, bf16[1,128,512]{2,1,0:T(8,128)(2,1)S(1)}, f32[5,8,512]{2,1,0:T(8,128)S(1)}) custom-call(s32[1,12]{1,0:T(1,128)} %counts_hbm.1, bf16[1,128,512]{2,1,0:T(8,128)(2,1)} %masters_hbm.1, bf16[1,128,512]{2,1,0:T(8,128)(2,1)} %cotan_hbm.1, s32[1,2048]{1,0:T(1,128)} %source_hbm.1, s32[1,2048]{1,0:T(1,128)} %target_hbm.1, ...), custom_call_target="tpu_custom_call" | custom-call | tf_op jit(solution)/shard_map/graph_conv_step/pallas_call | solution.py:523
  73.8 0.7 %handed_on.1 = (bf16[1,128,512]{2,1,0:T(8,128)(2,1)}, bf16[1,128,512]{2,1,0:T(8,128)(2,1)}, f32[5,8,512]{2,1,0:T(8,128)}) custom-call(bf16[1,128,512]{2,1,0:T(8,128)(2,1)S(1)} %get-tuple-element.6.refs_0_, bf16[1,128,512]{2,1,0:T(8,128)(2,1)S(1)} %get-tuple-element.7.refs_1_, f32[5,8,512]{2,1,0:T(8,128)S(1)} %get-tuple-element.8.refs_2_), custom_call_target="tpu_custom_call" | custom-call | tf_op jit(solution)/shard_map/handed_on/pallas_call | solution.py:537
